TPU v7x, 512 devices: a whole 4x8x8 slice. The times are simulated.
512 devices in a mesh: vocab: 64 (over y, x, core), grp: 8 (over z).
Axes of the slice: x: 4, y: 8, z: 8, core: 2. Of those that a mesh axis runs over, the one named last changes fastest.
Arguments:
- hidden: bfloat16 [2048, 4096], P('grp'), may hold values from -240 to 240
- head_weight: bfloat16 [4096, 32768], P('grp', 'vocab'), may hold values from -0.25 to 0.25
- cluster_weight: bfloat16 [4096, 3], replicated, may hold values from -0.5 to 0.5
- proj_one: bfloat16 [4096, 1024], P('vocab'), may hold values from -0.09375 to 0.09375
- proj_two: bfloat16 [4096, 256], P('vocab'), may hold values from -0.09375 to 0.09375
- proj_three: bfloat16 [4096, 64], P('vocab'), may hold values from -0.09375 to 0.09375
- tail_one: bfloat16 [1024, 65536], P('grp', 'vocab'), may hold values from -0.5 to 0.5
- tail_two: bfloat16 [256, 65536], P('grp', 'vocab'), may hold values from -1 to 1
- tail_three: bfloat16 [64, 65536], P('grp', 'vocab'), may hold values from -2 to 2
- targets: int32 [2048], P('grp'), may hold values from 0 to 229375, as said below
- flags: int32 [2048, 3], P('grp'), may hold values from 0 to 1, as said below
Outputs:
- target_logprob: float32 [2048], P('grp')
- tail_entropy: float32 [2048, 3], P('grp')
Inputs may be any that keep to these rules, and one draw needn't show every extreme that they name: `targets`: a target at or beyond 32768 lies in tail (t - 32768) // 65536. flags[b, c] is 1 whenever the target of sequence b lies in tail c.
All inputs are finite; a program needn't handle non-finite values.
Results may differ from a plain program's by a relative error of at most 0.0092.
Values may be sent and summed in bfloat16 or wider, within the bound.
No kernel may reach another device: no remote copies, remote signals or barrier semaphores. Data moves between devices by JAX's collectives and lax.ppermute only.
A program may use at most 64 MiB of HBM per device.

v0:
```python
import jax
import jax.numpy as jnp
from jax import lax
from jax.sharding import Mesh
from jax.sharding import PartitionSpec as P

V_HEAD = 32768
TAIL = 65536
VOCAB = ("vocab_0", "vocab_1", "vocab_2")


def split_up(shard, dim, size):
    dims = shard.shape
    pieces = shard.reshape(*dims[:dim], size, dims[dim] // size, *dims[dim + 1 :])
    return jnp.moveaxis(pieces, dim, 0)


def sent_and_summed(shard, axis, dim):
    pieces = split_up(shard, dim, lax.axis_size(axis))
    arrived = lax.all_to_all(pieces, axis, split_axis=0, concat_axis=0, tiled=True)
    return arrived.sum(axis=0)


def laid_out(pieces, dim):
    pieces = jnp.moveaxis(pieces, 0, dim)
    dims = pieces.shape
    return pieces.reshape(*dims[:dim], dims[dim] * dims[dim + 1], *dims[dim + 2 :])


def copy_for_each(shard, axis):
    copies = jnp.broadcast_to(shard, (lax.axis_size(axis), *shard.shape))
    return lax.all_to_all(copies, axis, split_axis=0, concat_axis=0, tiled=True)


def gathered_copies(shard, axis, dim):
    return laid_out(copy_for_each(shard, axis), dim)


def one_gather(arrays, axis, dims):
    vector = jnp.concatenate([a.reshape(-1) for a in arrays])
    lines, at, done = (lax.all_gather(vector, axis), 0, [])
    for a, dim in zip(arrays, dims):
        pieces = lines[:, at : at + a.size].reshape(-1, *a.shape)
        done.append(laid_out(pieces, dim))
        at += a.size
    return tuple(done)


def collected_together(shard, axis):
    leaves = jax.tree.leaves(shard)
    order = sorted(range(len(leaves)), key=lambda k: -leaves[k].size)
    width = (1, *leaves[order[0]].shape)[-1]
    lines = [
        jnp.pad(leaves[k].reshape(-1), (0, -leaves[k].size % width)).reshape(-1, width)
        for k in order
    ]
    both, at, found = (lax.all_gather(jnp.concatenate(lines), axis), 0, {})
    for k, line in zip(order, lines):
        share = both[:, at : at + len(line)].reshape(len(both), -1)
        found[k] = share[:, : leaves[k].size].reshape(-1, *leaves[k].shape)
        at += len(line)
    numbers = iter(range(len(leaves)))
    return jax.tree.map(lambda _: found[next(numbers)], shard)


def combined_by_axis(shard, axes, combine):
    for axis in axes:
        pieces = collected_together(shard, axis)
        shard = jax.tree.map(lambda part: part[0], pieces)
        for k in range(1, lax.axis_size(axis)):
            shard = combine(shard, jax.tree.map(lambda part: part[k], pieces))
    return shard


def combine_stats(first, second):
    head_max = jnp.maximum(first[0], second[0])
    head_sum = first[1] * jnp.exp(first[0] - head_max) + second[1] * jnp.exp(second[0] - head_max)
    tail_max = jnp.maximum(first[2], second[2])
    left = jnp.exp(first[2] - tail_max)
    right = jnp.exp(second[2] - tail_max)
    tail_sum = first[3] * left + second[3] * right
    tail_weighted = first[4] * left + second[4] * right
    return (head_max, head_sum, tail_max, tail_sum, tail_weighted, first[5] + second[5])


def shards(
    hidden,
    head_weight,
    cluster_weight,
    proj_one,
    proj_two,
    proj_three,
    tail_one,
    tail_two,
    tail_three,
    targets,
    flags,
):
    rows = hidden.shape[0]
    head_cols = head_weight.shape[1]
    vocab_index = lax.axis_index(VOCAB)
    head_logits = jnp.dot(
        hidden,
        lax.all_gather(head_weight, "grp", axis=0, tiled=True),
        preferred_element_type=jnp.float32,
    )
    cluster_score_logits = jnp.dot(hidden, cluster_weight, preferred_element_type=jnp.float32)
    width_voc = proj_one.shape[0]
    features = lax.dynamic_slice_in_dim(hidden, vocab_index * width_voc, width_voc, 1)
    joined_weight = jnp.concatenate((proj_one, proj_two, proj_three), axis=1)
    joined_partial_logits = jnp.dot(features, joined_weight, preferred_element_type=jnp.float32)
    share = sent_and_summed(joined_partial_logits, VOCAB, 1).astype(jnp.bfloat16)
    joined = gathered_copies(share, VOCAB, 1)
    first_end = proj_one.shape[1]
    second_end = first_end + proj_two.shape[1]
    projected = [joined[:, :first_end], joined[:, first_end:second_end], joined[:, second_end:]]
    full_tails = one_gather((tail_one, tail_two, tail_three), "grp", (0, 0, 0))
    tail_cluster_logits = jnp.stack(
        [
            jnp.dot(projected[index], full_tails[index], preferred_element_type=jnp.float32)
            for index in range(3)
        ],
        axis=0,
    )
    tail_cols = tail_cluster_logits.shape[2]
    head_ids = vocab_index * head_cols + jnp.arange(head_cols, dtype=jnp.int32)
    head_pick = jnp.sum(jnp.where(head_ids[None, :] == targets[:, None], head_logits, 0.0), axis=1)
    relative = targets - V_HEAD
    cluster = relative // TAIL
    word = relative - cluster * TAIL
    tail_ids = vocab_index * tail_cols + jnp.arange(tail_cols, dtype=jnp.int32)
    same_word = tail_ids[None, :] == word[:, None]
    tail_pick = jnp.zeros((rows,), jnp.float32)
    for index in range(3):
        hit = jnp.logical_and(same_word, (cluster == index)[:, None])
        tail_pick = tail_pick + jnp.sum(jnp.where(hit, tail_cluster_logits[index], 0.0), axis=1)
    picked = head_pick + tail_pick
    local_head_max = jnp.max(head_logits, axis=1)
    local_tail_max = jnp.transpose(jnp.max(tail_cluster_logits, axis=2))
    head_sum = jnp.sum(jnp.exp(head_logits - local_head_max[:, None]), axis=1)
    expo = jnp.exp(tail_cluster_logits - jnp.transpose(local_tail_max)[:, :, None])
    tail_sum = jnp.transpose(jnp.sum(expo, axis=2))
    tail_weighted = jnp.transpose(jnp.sum(expo * tail_cluster_logits, axis=2))
    merged = combined_by_axis(
        (local_head_max, head_sum, local_tail_max, tail_sum, tail_weighted, picked),
        VOCAB,
        combine_stats,
    )
    head_max, head_sum, tail_max, tail_sum, tail_weighted, picked = merged
    top = jnp.maximum(head_max, jnp.max(cluster_score_logits, axis=1))
    total = head_sum * jnp.exp(head_max - top) + jnp.sum(
        jnp.exp(cluster_score_logits - top[:, None]), axis=1
    )
    head_lse = top + jnp.log(total)
    tail_lse = tail_max + jnp.log(tail_sum)
    tail_mean = tail_weighted / tail_sum
    tail_entropy = flags.astype(jnp.float32) * (tail_lse - tail_mean)
    which = cluster[:, None] == jnp.arange(3, dtype=jnp.int32)[None, :]
    cluster_term = jnp.sum(jnp.where(which, cluster_score_logits - tail_lse, 0.0), axis=1)
    target_logprob = jnp.where(targets < V_HEAD, picked, picked + cluster_term) - head_lse
    return (target_logprob, tail_entropy)


def solution(mesh):
    finer = Mesh(
        mesh.devices.reshape(8, 4, 2, mesh.shape["grp"]), ("vocab_0", "vocab_1", "vocab_2", "grp")
    )
    in_specs = (
        P("grp", None),
        P("grp", VOCAB),
        P(),
        P(VOCAB, None),
        P(VOCAB, None),
        P(VOCAB, None),
        P("grp", VOCAB),
        P("grp", VOCAB),
        P("grp", VOCAB),
        P("grp"),
        P("grp", None),
    )
    out_specs = (P("grp"), P("grp", None))
    return jax.shard_map(
        shards, mesh=finer, in_specs=in_specs, out_specs=out_specs, check_vma=False
    )
```

profile of v0, /device:TPU:1, one launch (start us, length us, event | category | flops | bytes accessed | tf_op | source)
XLA Modules:
  0.0 180.4 jit_solution(7953923734584151872)
XLA Ops:
  7.2 0.9 copy.71
  8.1 0.8 copy.68
  8.9 1.0 copy.67
  9.9 0.8 pad_maximum_fusion.1
  10.8 0.7 all-gather.10.cloned.1.call-update
  11.5 1.4 fusion.4
  12.9 1.3 reshape.130
  14.2 50.8 %all_to_all.10 = f32[64,256,21]{1,2,0:T(8,128)} all-to-all(f32[64,256,21]{1,2,0:T(8,128)} %bitcast.526), channel_id=1, replica_groups=mesh['vocab_0'=8,'vocab_1'=4,'vocab_2'=2,'grp'=8] {'vocab_0','vocab_1','..., dimensions={0} | all-to-all | bytes 2752512 | tf_op jit(solution)/shard_map/all_to_all | solution.py:20
  65.1 1.5 reduce_sum.90
  66.6 0.9 broadcast_in_dim.15
  67.5 6.4 %all-to-all-start.1 = ((bf16[64,256,21]{1,2,0:T(8,128)(2,1)}), bf16[64,256,21]{1,2,0:T(8,128)(2,1)S(1)}, u32[]{:S(2)}, u32[]{:S(2)}) async-start(bf16[64,256,21]{1,2,0:T(8,128)(2,1)} %broadcast_in_dim.15), calls=%async_computation.1 | async-start | bytes 1572864 | tf_op jit(solution)/shard_map/all_to_all | solution.py:32
  74.0 0.7 fusion.112
  74.7 22.2 %all-to-all-done.1 = bf16[64,256,21]{1,2,0:T(8,128)(2,1)S(1)} async-done(((bf16[64,256,21]{1,2,0:T(8,128)(2,1)}), bf16[64,256,21]{1,2,0:T(8,128)(2,1)S(1)}, u32[]{:S(2)}, u32[]{:S(2)}) %all-to-all-start.1) | async-done | bytes 688160 | tf_op jit(solution)/shard_map/all_to_all | solution.py:32
  97.0 1.1 reshape.131
  98.0 4.6 %reshape.156 = bf16[8,172032]{1,0:T(8,128)(2,1)} reshape(bf16[1376256]{0:T(1024)(128)(2,1)} %all-gather.12.cloned.1.call-done) | data formatting | bytes 5505024 | tf_op jit(solution)/shard_map/all_gather | solution.py:41
  102.6 3.1 %slice.499 = bf16[8,131072]{1,0:T(8,128)(2,1)} slice(bf16[8,172032]{1,0:T(8,128)(2,1)} %reshape.156), slice={[0:8], [0:131072]} | slice | bytes 4194304 | tf_op jit(solution)/shard_map/slice | solution.py:43
  105.7 0.7 reshape_reshape.11
  106.4 3.9 %reshape_reshape.9 = bf16[1024,1024]{1,0:T(8,128)(2,1)} reshape(bf16[8,131072]{1,0:T(8,128)(2,1)} %slice.499) | data formatting | bytes 4194304 | tf_op jit(solution)/shard_map/reshape;reshape | solution.py:27
  110.4 1.0 reshape_reshape.10
  111.4 0.3 fusion.14
  111.7 2.3 %fusion.2 = f32[256,1024]{1,0:T(8,128)S(1)} fusion(bf16[1024,1024]{1,0:T(8,128)(2,1)} %reshape_reshape.9, bf16[256,1344]{0,1:T(8,128)(2,1)S(1)} %copy-done.1), kind=kOutput, calls=%fused_computation.11 | convolution fusion | flops 536870912 | bytes 3670016 | tf_op jit(solution)/shard_map/dot_general | solution.py:120
  114.1 0.8 select_reduce_fusion.1
  114.8 0.2 fusion.1
  115.0 0.9 multiply_reduce_fusion
  115.9 5.0 %all-gather.10.cloned.1.call-done = bf16[4096,512]{1,0:T(8,128)(2,1)} async-done(((bf16[512,512]{1,0:T(8,128)(2,1)}), bf16[4096,512]{1,0:T(8,128)(2,1)}) %all-gather.10.cloned.1.call-update) | async-done | bytes 4194320 | tf_op jit(solution)/shard_map/all_gather | solution.py:104
  120.9 3.5 %fusion.111 = (f32[256]{0:T(256)S(1)}, f32[256,512]{1,0:T(8,128)S(1)}) fusion(bf16[256,4096]{1,0:T(8,128)(2,1)S(1)} %copy-done, bf16[4096,512]{1,0:T(8,128)(2,1)} %all-gather.10.cloned.1.call-done), kind=kOutput, calls=%fused_computation.231 | convolution fusion | flops 1073872640 | bytes 6816768 | tf_op jit(solution)/shard_map/dot_general | solution.py:102
  124.4 0.3 select_reduce_fusion.3
  124.8 0.2 reshape.136
  124.9 0.1 copy.50
  125.0 0.2 reshape.135
  125.2 0.1 copy.49
  125.3 0.2 reshape.137
  125.5 0.1 concatenate.17
  125.6 19.9 %all-gather.4 = f32[8,1026,3]{1,2,0:T(4,128)S(1)} all-gather(f32[1,1026,3]{1,2,0:T(4,128)S(1)} %bitcast.534), channel_id=3, replica_groups=mesh['vocab_0'=8,'vocab_1'=4,'vocab_2'=2,'grp'=8] {'vocab_0'}, dimensions={0}, use_global_device_ids=true | all-gather | bytes 110808 | tf_op jit(solution)/shard_map/all_gather | solution.py:57
  145.6 0.1 fusion.104
  145.6 0.2 copy.54
  145.9 0.4 fusion.10
  146.3 0.2 reshape.143
  146.5 0.2 copy.53
  146.8 0.1 copy.52
  147.0 1.1 slice_reduce_fusion.7
  148.2 0.2 reshape.139
  148.4 0.2 reshape.141
  148.7 0.1 concatenate.18
  148.8 9.3 %all-gather.5 = f32[4,1026,3]{1,2,0:T(4,128)S(1)} all-gather(f32[1,1026,3]{1,2,0:T(4,128)S(1)} %bitcast.535), channel_id=4, replica_groups=mesh['vocab_0'=8,'vocab_1'=4,'vocab_2'=2,'grp'=8] {'vocab_1'}, dimensions={0}, use_global_device_ids=true | all-gather | bytes 61560 | tf_op jit(solution)/shard_map/all_gather | solution.py:57
  158.2 0.1 copy.60
  158.4 0.2 reshape.148
  158.6 0.2 reshape.149
  158.8 0.2 copy.59
  159.0 0.2 reshape.146
  159.2 0.1 copy.58
  159.3 0.2 reshape.144
  159.6 0.2 reshape.145
  159.8 0.2 reshape.147
  160.1 0.1 concatenate.19
  160.2 11.1 %all-gather.6 = f32[2,1026,3]{1,2,0:T(4,128)S(1)} all-gather(f32[1,1026,3]{1,2,0:T(4,128)S(1)} %bitcast.533), channel_id=5, replica_groups=mesh['vocab_0'=8,'vocab_1'=4,'vocab_2'=2,'grp'=8] {'vocab_2'}, dimensions={0}, use_global_device_ids=true | all-gather | bytes 36936 | tf_op jit(solution)/shard_map/all_gather | solution.py:57
  171.4 0.1 copy.66
  171.5 0.2 reshape.152
  171.7 0.1 copy.65
  171.8 0.2 reshape.151
  172.0 0.1 copy.64
  172.1 0.2 reshape.150
  172.3 0.6 exponential_reduce_fusion.1
  173.0 0.6 fusion.95
  (64 shorter events, 1.3 us)
Async XLA Ops:
  7.2 4.3 %copy-start = (bf16[256,4096]{1,0:T(8,128)(2,1)S(1)}, bf16[256,4096]{1,0:T(8,128)(2,1)}, u32[]{:S(2)}) copy-start(bf16[256,4096]{1,0:T(8,128)(2,1)} %param.11) | copy-start | bytes 6291460
  7.2 90.9 %all-gather.12.cloned.1.call-start = ((), (), s32[]{:S(2)}) async-start(), calls=%async_computation.3 | async-start | bytes 3096576 | tf_op jit(solution)/shard_map/all_gather | solution.py:41
  10.7 110.2 %all-gather.10.cloned.1.call-start = ((), (), s32[]{:S(2)}) async-start(), calls=%async_computation.2 | async-start | bytes 4718592 | tf_op jit(solution)/shard_map/all_gather | solution.py:104
  65.1 8.9 %copy-start.5 = (s32[256]{0:T(256)S(1)}, s32[256]{0:T(256)}, u32[]{:S(2)}) copy-start(s32[256]{0:T(256)} %param.20) | copy-start | bytes 3076
  65.1 9.0 %copy-start.4 = (bf16[4096,3]{0,1:T(4,128)(2,1)S(1)}, bf16[4096,3]{0,1:T(4,128)(2,1)}, u32[]{:S(2)}) copy-start(bf16[4096,3]{0,1:T(4,128)(2,1)} %param.13) | copy-start | bytes 73732
  67.5 29.4 %all-to-all-start.1 = ((bf16[64,256,21]{1,2,0:T(8,128)(2,1)}), bf16[64,256,21]{1,2,0:T(8,128)(2,1)S(1)}, u32[]{:S(2)}, u32[]{:S(2)}) async-start(bf16[64,256,21]{1,2,0:T(8,128)(2,1)} %broadcast_in_dim.15), calls=%async_computation.1 | async-start | bytes 1572864 | tf_op jit(solution)/shard_map/all_to_all | solution.py:32
  102.6 3.1 %slice-start = ((bf16[8,172032]{1,0:T(8,128)(2,1)}), bf16[8,8192]{1,0:T(8,128)(2,1)S(1)}, s32[]{:S(2)}) async-start(bf16[8,172032]{1,0:T(8,128)(2,1)} %reshape.156), calls=%async_computation.4 | async-start | bytes 262144 | tf_op jit(solution)/shard_map/slice | solution.py:43
  105.7 4.6 %slice-start.1 = ((bf16[8,172032]{1,0:T(8,128)(2,1)}), bf16[8,32768]{1,0:T(8,128)(2,1)S(1)}, s32[]{:S(2)}) async-start(bf16[8,172032]{1,0:T(8,128)(2,1)} %reshape.156), calls=%async_computation.5 | async-start | bytes 1048576 | tf_op jit(solution)/shard_map/slice | solution.py:43
  105.7 5.7 %copy-start.1 = (bf16[256,1344]{0,1:T(8,128)(2,1)S(1)}, bf16[256,1344]{0,1:T(8,128)(2,1)}, u32[]{:S(2)}) copy-start(bf16[256,1344]{0,1:T(8,128)(2,1)} %reshape.131) | copy-start | bytes 2064388
  106.4 5.0 %copy-start.2 = (bf16[64,1024]{1,0:T(8,128)(2,1)S(1)}, bf16[64,1024]{1,0:T(8,128)(2,1)}, u32[]{:S(2)}) copy-start(bf16[64,1024]{1,0:T(8,128)(2,1)} %reshape_reshape.11) | copy-start | bytes 393220
  111.4 2.6 %copy-start.3 = (bf16[256,1024]{1,0:T(8,128)(2,1)S(1)}, bf16[256,1024]{1,0:T(8,128)(2,1)}, u32[]{:S(2)}) copy-start(bf16[256,1024]{1,0:T(8,128)(2,1)} %reshape_reshape.10) | copy-start | bytes 1572868
  146.7 25.6 %copy-start.6 = (s32[256,3]{0,1:T(4,128)S(1)}, s32[256,3]{0,1:T(4,128)}, u32[]{:S(2)}) copy-start(s32[256,3]{0,1:T(4,128)} %param.21) | copy-start | bytes 9220
Sparse Core Ops, SparseCore 0:
  10.8 48.8 all-gather.11
  61.8 59.1 all-gather.9
where the time goes:
time: 181 us; the launch traced here: 180 us
  blocking collectives  91.2 us (50%)
  waiting for transfers between devices  27.9 us (15%)
  local copies, waits for them, and re-layouts  25.9 us (14%)
  between operations  14.4 us (8%)
  matrix products  8.93 us (5%)
  starting transfers between devices  6.48 us (4%)
  other arithmetic  5.55 us (3%)
    all_to_all x1, blocking collectives, sent_and_summed(): lax.all_to_all(pieces, axis, split_axis=0, concat_axis=0, tiled=True)  50.8 us
    all_gather x3, blocking collectives, collected_together(): both, at, found = (lax.all_gather(jnp.concatenate(lines), axis), 0, {})  40.3 us
    all_to_all x1, waiting for transfers between devices, copy_for_each(): return lax.all_to_all(copies, axis, split_axis=0, concat_axis=0, tiled=True)  22.2 us
    all_to_all x1, starting transfers between devices, copy_for_each(): return lax.all_to_all(copies, axis, split_axis=0, concat_axis=0, tiled=True)  6.4 us
    another operation x3, local copies, waits for them, and re-layouts, laid_out(): pieces.reshape(*dims[:dim], dims[dim] * dims[dim + 1], *dims[dim + 2:])  5.69 us
    all_gather x1, waiting for transfers between devices, shards(): lax.all_gather(head_weight, 'grp', axis=0, tiled=True)  4.98 us
    all_gather x1, local copies, waits for them, and re-layouts, one_gather(): lines, at, done = (lax.all_gather(vector, axis), 0, [])  4.56 us
  transfers between devices with their start and end apart: 3, of which 2 were waited for; matrix products, arithmetic and copies ran while one was open for 14% of the time, Pallas kernels for 0%

commit v1 on v0

--- a/solution.py
+++ b/solution.py
@@ -1,3 +1,4 @@
+import functools
 import jax
 import jax.numpy as jnp
 from jax import lax
@@ -7,6 +8,21 @@
 V_HEAD = 32768
 TAIL = 65536
 VOCAB = ("vocab_0", "vocab_1", "vocab_2")
+
+
+def _choose_waves(inp, net_axis):
+    return jnp.concatenate(
+        lax.all_to_all(
+            jnp.stack(tuple((inp for _ in range(lax.psum(1, axis_name=net_axis)))), 0),
+            axis_name=net_axis,
+            split_axis=0,
+            concat_axis=0,
+        ),
+        0,
+    )
+
+
+set_the_pairs_all = functools.partial(_choose_waves, net_axis="grp")
 
 
 def split_up(shard, dim, size):
@@ -100,9 +116,7 @@
     head_cols = head_weight.shape[1]
     vocab_index = lax.axis_index(VOCAB)
     head_logits = jnp.dot(
-        hidden,
-        lax.all_gather(head_weight, "grp", axis=0, tiled=True),
-        preferred_element_type=jnp.float32,
+        hidden, set_the_pairs_all(head_weight), preferred_element_type=jnp.float32
     )
     cluster_score_logits = jnp.dot(hidden, cluster_weight, preferred_element_type=jnp.float32)
     width_voc = proj_one.shape[0]

time: 181 us -> 298 us (1.65)
  the two profiles are of different devices: /device:TPU:1 before, /device:TPU:257 now
where the time goes in v1:
time: 298 us; the launch traced here: 297 us
  waiting for transfers between devices  126 us (42%)
  blocking collectives  102 us (34%)
  local copies, waits for them, and re-layouts  28.2 us (9%)
  between operations  14.5 us (5%)
  starting transfers between devices  13.2 us (4%)
  matrix products  8.93 us (3%)
  other arithmetic  5.58 us (2%)
    all_gather x1, waiting for transfers between devices, one_gather(): lines, at, done = (lax.all_gather(vector, axis), 0, [])  103 us
    all_gather x3, blocking collectives, collected_together(): both, at, found = (lax.all_gather(jnp.concatenate(lines), axis), 0, {})  51.6 us
    all_to_all x1, blocking collectives, sent_and_summed(): lax.all_to_all(pieces, axis, split_axis=0, concat_axis=0, tiled=True)  50 us
    all_to_all x1, waiting for transfers between devices, copy_for_each(): return lax.all_to_all(copies, axis, split_axis=0, concat_axis=0, tiled=True)  22.9 us
    all_to_all x1, starting transfers between devices, _choose_waves(): lax.all_to_all(jnp.stack(tuple((inp for _ in range(lax.psum(1, axis_name=...  6.81 us
    all_to_all x1, starting transfers between devices, copy_for_each(): return lax.all_to_all(copies, axis, split_axis=0, concat_axis=0, tiled=True)  6.37 us
  transfers between devices with their start and end apart: 3, of which 2 were waited for; matrix products, arithmetic and copies ran while one was open for 7% of the time, Pallas kernels for 0%

profile of v1, /device:TPU:257, one launch (start us, length us, event | category | flops | bytes accessed | tf_op | source)
XLA Modules:
  0.0 297.5 jit_solution(3328314030173060069)
XLA Ops:
  7.2 1.6 copy-done
  8.8 1.4 fusion.4
  10.1 1.3 reshape.135
  11.5 50.0 %all_to_all.15 = f32[64,256,21]{1,2,0:T(8,128)} all-to-all(f32[64,256,21]{1,2,0:T(8,128)} %bitcast.527), channel_id=1, replica_groups=mesh['vocab_0'=8,'vocab_1'=4,'vocab_2'=2,'grp'=8] {'vocab_0','vocab_1','..., dimensions={0} | all-to-all | bytes 2752512 | tf_op jit(solution)/shard_map/all_to_all | solution.py:36
  61.4 1.6 reduce_sum.90
  63.0 0.9 broadcast_in_dim.15
  63.9 6.4 %all-to-all-start.1 = ((bf16[64,256,21]{1,2,0:T(8,128)(2,1)}), bf16[64,256,21]{1,2,0:T(8,128)(2,1)S(1)}, u32[]{:S(2)}, u32[]{:S(2)}) async-start(bf16[64,256,21]{1,2,0:T(8,128)(2,1)} %broadcast_in_dim.15), calls=%async_computation.1 | async-start | bytes 1572864 | tf_op jit(solution)/shard_map/all_to_all | solution.py:48
  70.4 22.9 %all-to-all-done.1 = bf16[64,256,21]{1,2,0:T(8,128)(2,1)S(1)} async-done(((bf16[64,256,21]{1,2,0:T(8,128)(2,1)}), bf16[64,256,21]{1,2,0:T(8,128)(2,1)S(1)}, u32[]{:S(2)}, u32[]{:S(2)}) %all-to-all-start.1) | async-done | bytes 688160 | tf_op jit(solution)/shard_map/all_to_all | solution.py:48
  93.3 3.4 %stack.27 = bf16[8,512,512]{2,1,0:T(8,128)(2,1)} broadcast(bf16[512,512]{1,0:T(8,128)(2,1)} %param.12), dimensions={1,2} | broadcast | bytes 4718592 | tf_op jit(solution)/shard_map/stack | solution.py:16
  96.7 6.8 %all-to-all-start.2 = ((bf16[8,512,512]{2,1,0:T(8,128)(2,1)}), bf16[8,512,512]{2,1,0:T(8,128)(2,1)}, u32[]{:S(2)}, u32[]{:S(2)}) async-start(bf16[8,512,512]{2,1,0:T(8,128)(2,1)} %stack.27), calls=%async_computation.2 | async-start | bytes 8388608 | tf_op jit(solution)/shard_map/all_to_all | solution.py:15
  103.5 0.7 pad_maximum_fusion.1
  104.4 0.7 fusion.112
  105.0 1.1 reshape.136
  106.2 102.7 %all-gather.9.cloned.1.call-done = bf16[1376256]{0:T(1024)(128)(2,1)} async-done(((bf16[172032]{0:T(1024)(128)(2,1)}), bf16[1376256]{0:T(1024)(128)(2,1)}) %all-gather.9.cloned.1.call-update) | async-done | bytes 2752528 | tf_op jit(solution)/shard_map/all_gather | solution.py:57
  208.8 4.6 %reshape.162 = bf16[8,172032]{1,0:T(8,128)(2,1)} reshape(bf16[1376256]{0:T(1024)(128)(2,1)} %all-gather.9.cloned.1.call-done) | data formatting | bytes 5505024 | tf_op jit(solution)/shard_map/all_gather | solution.py:57
  213.4 3.1 %slice.499 = bf16[8,131072]{1,0:T(8,128)(2,1)} slice(bf16[8,172032]{1,0:T(8,128)(2,1)} %reshape.162), slice={[0:8], [0:131072]} | slice | bytes 4194304 | tf_op jit(solution)/shard_map/slice | solution.py:59
  216.5 0.7 reshape_reshape.11
  217.2 3.9 %reshape_reshape.9 = bf16[1024,1024]{1,0:T(8,128)(2,1)} reshape(bf16[8,131072]{1,0:T(8,128)(2,1)} %slice.499) | data formatting | bytes 4194304 | tf_op jit(solution)/shard_map/reshape;reshape | solution.py:43
  221.1 1.1 reshape_reshape.10
  222.2 0.3 fusion.14
  222.5 2.3 fusion.2
  224.8 0.8 select_reduce_fusion.1
  225.6 0.2 fusion.1
  225.8 0.9 multiply_reduce_fusion
  226.7 3.5 %fusion.111 = (f32[256]{0:T(256)S(1)}, f32[256,512]{1,0:T(8,128)S(1)}) fusion(bf16[256,4096]{1,0:T(8,128)(2,1)S(1)} %copy-done, bf16[4096,512]{1,0:T(8,128)(2,1)} %bitcast.8), kind=kOutput, calls=%fused_computation.231 | convolution fusion | flops 1073872640 | bytes 6816768 | tf_op jit(solution)/shard_map/dot_general | solution.py:118
  230.2 0.3 select_reduce_fusion.3
  230.6 0.2 reshape.142
  230.8 0.2 reshape.141
  231.1 0.2 reshape.143
  231.3 0.1 concatenate.17
  231.4 31.5 %all-gather.4 = f32[8,1026,3]{1,2,0:T(4,128)S(1)} all-gather(f32[1,1026,3]{1,2,0:T(4,128)S(1)} %bitcast.535), channel_id=3, replica_groups=mesh['vocab_0'=8,'vocab_1'=4,'vocab_2'=2,'grp'=8] {'vocab_0'}, dimensions={0}, use_global_device_ids=true | all-gather | bytes 110808 | tf_op jit(solution)/shard_map/all_gather | solution.py:73
  262.9 0.1 fusion.104
  263.0 0.2 copy.54
  263.3 0.4 fusion.10
  263.6 0.2 reshape.149
  263.8 0.1 copy.57
  263.9 0.2 copy.53
  264.1 0.1 copy.52
  264.4 1.1 slice_reduce_fusion.7
  265.6 0.2 reshape.145
  265.7 0.1 copy.55
  265.8 0.2 reshape.147
  266.0 0.1 copy.56
  266.1 0.1 concatenate.18
  266.2 9.0 %all-gather.5 = f32[4,1026,3]{1,2,0:T(4,128)S(1)} all-gather(f32[1,1026,3]{1,2,0:T(4,128)S(1)} %bitcast.536), channel_id=4, replica_groups=mesh['vocab_0'=8,'vocab_1'=4,'vocab_2'=2,'grp'=8] {'vocab_1'}, dimensions={0}, use_global_device_ids=true | all-gather | bytes 61560 | tf_op jit(solution)/shard_map/all_gather | solution.py:73
  275.3 0.1 copy.60
  275.5 0.2 reshape.154
  275.7 0.2 reshape.155
  275.9 0.2 copy.59
  276.1 0.2 reshape.152
  276.3 0.1 copy.58
  276.4 0.2 reshape.150
  276.7 0.2 reshape.151
  276.9 0.2 reshape.153
  277.1 0.1 concatenate.19
  277.2 11.1 %all-gather.6 = f32[2,1026,3]{1,2,0:T(4,128)S(1)} all-gather(f32[1,1026,3]{1,2,0:T(4,128)S(1)} %bitcast.534), channel_id=5, replica_groups=mesh['vocab_0'=8,'vocab_1'=4,'vocab_2'=2,'grp'=8] {'vocab_2'}, dimensions={0}, use_global_device_ids=true | all-gather | bytes 36936 | tf_op jit(solution)/shard_map/all_gather | solution.py:73
  288.4 0.1 copy.66
  288.6 0.2 reshape.158
  288.8 0.1 copy.65
  288.9 0.2 reshape.157
  289.1 0.1 copy.64
  289.2 0.2 reshape.156
  289.4 0.6 exponential_reduce_fusion.1
  290.0 0.6 fusion.95
  (70 shorter events, 1.3 us)
Async XLA Ops:
  7.2 1.6 copy-start
  61.4 8.9 %copy-start.8 = (bf16[8,1024]{1,0:T(8,128)(2,1)S(1)}, bf16[8,1024]{1,0:T(8,128)(2,1)}, u32[]{:S(2)}) copy-start(bf16[8,1024]{1,0:T(8,128)(2,1)} %param.19) | copy-start | bytes 49156
  61.4 8.9 %copy-start.5 = (bf16[32,1024]{1,0:T(8,128)(2,1)S(1)}, bf16[32,1024]{1,0:T(8,128)(2,1)}, u32[]{:S(2)}) copy-start(bf16[32,1024]{1,0:T(8,128)(2,1)} %param.18) | copy-start | bytes 196612
  61.4 8.9 %copy-start.4 = (bf16[128,1024]{1,0:T(8,128)(2,1)S(1)}, bf16[128,1024]{1,0:T(8,128)(2,1)}, u32[]{:S(2)}) copy-start(bf16[128,1024]{1,0:T(8,128)(2,1)} %param.17) | copy-start | bytes 786436
  63.9 29.4 %all-to-all-start.1 = ((bf16[64,256,21]{1,2,0:T(8,128)(2,1)}), bf16[64,256,21]{1,2,0:T(8,128)(2,1)S(1)}, u32[]{:S(2)}, u32[]{:S(2)}) async-start(bf16[64,256,21]{1,2,0:T(8,128)(2,1)} %broadcast_in_dim.15), calls=%async_computation.1 | async-start | bytes 1572864 | tf_op jit(solution)/shard_map/all_to_all | solution.py:48
  96.7 7.6 %copy-start.7 = (s32[256]{0:T(256)S(1)}, s32[256]{0:T(256)}, u32[]{:S(2)}) copy-start(s32[256]{0:T(256)} %param.20) | copy-start | bytes 3076
  96.7 7.7 %copy-start.6 = (bf16[4096,3]{0,1:T(4,128)(2,1)S(1)}, bf16[4096,3]{0,1:T(4,128)(2,1)}, u32[]{:S(2)}) copy-start(bf16[4096,3]{0,1:T(4,128)(2,1)} %param.13) | copy-start | bytes 73732
  96.7 130.0 %all-to-all-start.2 = ((bf16[8,512,512]{2,1,0:T(8,128)(2,1)}), bf16[8,512,512]{2,1,0:T(8,128)(2,1)}, u32[]{:S(2)}, u32[]{:S(2)}) async-start(bf16[8,512,512]{2,1,0:T(8,128)(2,1)} %stack.27), calls=%async_computation.2 | async-start | bytes 8388608 | tf_op jit(solution)/shard_map/all_to_all | solution.py:15
  103.5 105.3 %all-gather.9.cloned.1.call-start = ((), (), s32[]{:S(2)}) async-start(), calls=%async_computation.3 | async-start | bytes 3096576 | tf_op jit(solution)/shard_map/all_gather | solution.py:57
  213.4 3.1 %slice-start = ((bf16[8,172032]{1,0:T(8,128)(2,1)}), bf16[8,8192]{1,0:T(8,128)(2,1)S(1)}, s32[]{:S(2)}) async-start(bf16[8,172032]{1,0:T(8,128)(2,1)} %reshape.162), calls=%async_computation.4 | async-start | bytes 262144 | tf_op jit(solution)/shard_map/slice | solution.py:59
  216.4 4.7 %slice-start.1 = ((bf16[8,172032]{1,0:T(8,128)(2,1)}), bf16[8,32768]{1,0:T(8,128)(2,1)S(1)}, s32[]{:S(2)}) async-start(bf16[8,172032]{1,0:T(8,128)(2,1)} %reshape.162), calls=%async_computation.5 | async-start | bytes 1048576 | tf_op jit(solution)/shard_map/slice | solution.py:59
  216.4 5.7 %copy-start.1 = (bf16[256,1344]{0,1:T(8,128)(2,1)S(1)}, bf16[256,1344]{0,1:T(8,128)(2,1)}, u32[]{:S(2)}) copy-start(bf16[256,1344]{0,1:T(8,128)(2,1)} %reshape.136) | copy-start | bytes 2064388
  217.2 5.0 %copy-start.2 = (bf16[64,1024]{1,0:T(8,128)(2,1)S(1)}, bf16[64,1024]{1,0:T(8,128)(2,1)}, u32[]{:S(2)}) copy-start(bf16[64,1024]{1,0:T(8,128)(2,1)} %reshape_reshape.11) | copy-start | bytes 393220
  222.2 2.6 copy-start.3
  264.1 25.3 %copy-start.9 = (s32[256,3]{0,1:T(4,128)S(1)}, s32[256,3]{0,1:T(4,128)}, u32[]{:S(2)}) copy-start(s32[256,3]{0,1:T(4,128)} %param.21) | copy-start | bytes 9220
Sparse Core Ops, SparseCore 0:
  106.4 102.3 all-gather.8
